TPU v7x, 32 devices: a whole 2x2x4 slice. The times are simulated.
32 devices in a mesh: cuts: 2 (over y), blk: 4 (over z), sol: 4 (over x, core).
Axes of the slice: x: 2, y: 2, z: 4, core: 2. Of those that a mesh axis runs over, the one named last changes fastest.
Arguments:
- solutions: bfloat16 [20, 2, 3, 256, 4096], P('cuts', None, None, None, ('blk', 'sol')), parts along dimension 0, may hold values from -6 to 6
- eigvecs: bfloat16 [20, 2, 3, 128, 4096], P('cuts', None, None, None, ('blk', 'sol')), parts along dimension 0, may hold values from -430 to 430
Outputs:
- projected: float32 [128, 20, 2, 256], P(('blk', 'sol'), 'cuts'), parts along dimension 1
There are 2 independent parts, one for each index of `cuts`. A program takes and returns all parts, laid end to end along the dimension named above; each array names one. Nothing has to cross between parts.
All inputs are finite; a program needn't handle non-finite values.
Results may differ from a plain program's by a relative error of at most 0.0003.
Values sent between devices are 32-bit elements; how exact they have to be, the bound alone decides.
A program may use at most 64 MiB of HBM per device.

v0:
```python
import jax
import jax.numpy as jnp
from jax import lax
from jax.sharding import PartitionSpec as P


def shards(solutions, eigvecs):
    blocks = lax.axis_size("blk")
    within = lax.axis_size("sol")
    slices, _, _, total_rows, local_sites = eigvecs.shape
    sumsq = jnp.sum(jnp.square(eigvecs.astype(jnp.float32)), axis=(1, 2, 4))
    totals = lax.psum(sumsq, ("blk", "sol"))
    floor_value = jnp.float32(local_sites * blocks * within)
    scale = lax.rsqrt(jnp.maximum(totals, floor_value))
    own_rows = total_rows // (blocks * within)
    real = jnp.einsum("trckx,trcnx->ktn", eigvecs, solutions, preferred_element_type=jnp.float32)
    imag = jnp.einsum(
        "tckx,tcnx->ktn", eigvecs[:, 0], solutions[:, 1], preferred_element_type=jnp.float32
    )
    imag = imag - jnp.einsum(
        "tckx,tcnx->ktn", eigvecs[:, 1], solutions[:, 0], preferred_element_type=jnp.float32
    )
    summed = lax.psum_scatter(
        jnp.stack((real, imag), axis=2), ("blk", "sol"), scatter_dimension=0, tiled=True
    )
    owner = lax.axis_index("blk") * within + lax.axis_index("sol")
    mine = lax.dynamic_slice_in_dim(scale, owner * own_rows, own_rows, 1)
    return summed * jnp.transpose(mine)[:, :, None, None]


def solution(mesh):
    in_specs = (
        P("cuts", None, None, None, ("blk", "sol")),
        P("cuts", None, None, None, ("blk", "sol")),
    )
    out_specs = P(("blk", "sol"), "cuts", None, None)
    return jax.shard_map(shards, mesh=mesh, in_specs=in_specs, out_specs=out_specs, check_vma=False)
```

profile of v0, /device:TPU:0, one launch (start us, length us, event | category | flops | bytes accessed | tf_op | source)
XLA Modules:
  0.0 131.8 jit_solution(10245911070047044523)
XLA Ops:
  6.5 0.0 all-reduce.3.cloned.1.call-start
  6.5 0.0 copy-start
  6.5 0.0 copy-start.1
  6.5 4.1 %fusion.2 = f32[10,256,128]{2,1,0:T(8,128)S(1)} fusion(bf16[10,2,3,256,256]{4,3,2,1,0:T(8,128)(2,1)} %param.2, bf16[10,2,3,128,256]{4,3,2,1,0:T(8,128)(2,1)} %param.3), kind=kOutput, calls=%fused_computation.8 | convolution fusion | flops 503316480 | bytes 7208960 | tf_op jit(solution)/shard_map/tckx,tcnx->ktn/dot_general | solution.py:17
  10.6 0.0 copy-done
  10.6 2.1 %copy-done.1 = bf16[10,2,3,256,256]{4,3,2,1,0:T(8,128)(2,1)S(1)} copy-done((bf16[10,2,3,256,256]{4,3,2,1,0:T(8,128)(2,1)S(1)}, bf16[10,2,3,256,256]{4,3,2,1,0:T(8,128)(2,1)}, u32[]{:S(2)}) %copy-start.1) | copy-done | bytes 7864344
  12.7 2.2 %convolution_bitcast_fusion = f32[128,10,1,256]{0,3,1,2:T(8,128)S(1)} fusion(bf16[10,2,3,128,256]{4,3,2,1,0:T(8,128)(2,1)S(1)} %copy-done, bf16[10,2,3,256,256]{4,3,2,1,0:T(8,128)(2,1)S(1)} %copy-done.1), kind=kOutput, calls=%fused_computation.10 | convolution fusion | flops 1006632960 | bytes 13107200 | tf_op jit(solution)/shard_map/trckx,trcnx->ktn/dot_general | solution.py:16
  14.9 1.2 fusion.5
  16.1 0.2 pad_maximum_fusion
  16.3 3.2 %copy.23 = f32[128,10,2,256]{3,2,1,0:T(2,128)} copy(f32[128,10,2,256]{0,3,1,2:T(8,128)S(1)} %pad_maximum_fusion) | data formatting | bytes 5242880 | tf_op jit(solution)/shard_map/stack | solution.py:24
  19.5 0.0 copy-start.2
  19.5 0.0 all-reduce.3.cloned.1.call-update
  19.6 3.0 %multiply_reduce_fusion = f32[10,128]{1,0:T(8,128)S(1)} fusion(bf16[10,2,3,128,256]{4,3,2,1,0:T(8,128)(2,1)} %param.3), kind=kLoop, calls=%fused_computation | loop fusion | flops 5896960 | bytes 3937280 | tf_op jit(solution)/shard_map/reduce_sum | solution.py:11
  22.5 36.2 %psum.7 = f32[10,128]{1,0:T(8,128)S(1)} all-reduce(f32[10,128]{1,0:T(8,128)S(1)} %multiply_reduce_fusion), channel_id=1, replica_groups=mesh['cuts'=2,'blk'=4,'sol'=4] {'blk','sol'}, use_global_device_ids=true, to_apply=%region_2.0 | all-reduce | flops 1280 | bytes 10240 | tf_op jit(solution)/shard_map/psum | solution.py:12
  58.7 0.1 fusion.7
  58.8 0.1 copy.24
  58.9 0.0 copy-done.2
  58.9 0.6 dynamic-slice
  60.1 63.1 %all-reduce.3.cloned.1.call-done = f32[128,10,2,256]{3,2,1,0:T(2,128)} async-done(((f32[128,10,2,256]{3,2,1,0:T(2,128)}), f32[128,10,2,256]{3,2,1,0:T(2,128)}) %all-reduce.3.cloned.1.call-update) | async-done | bytes 2621456
  123.2 1.7 %dynamic-slice_multiply_fusion = f32[8,10,2,256]{3,2,1,0:T(2,128)} fusion(f32[128,10,2,256]{3,2,1,0:T(2,128)} %all-reduce.3.cloned.1.call-done, u32[]{:T(128)S(6)} %multiply.1, f32[8,10]{1,0:T(8,128)S(1)} %copy.24), kind=kLoop, calls=%fused_computation.13 | loop fusion | flops 40960 | bytes 328004 | tf_op jit(solution)/shard_map/mul | solution.py:28
Async XLA Ops:
  6.5 116.7 %all-reduce.3.cloned.1.call-start = ((), (), s32[]{:S(2)}) async-start(), calls=%async_computation | async-start | bytes 5242880
  6.5 4.1 %copy-start = (bf16[10,2,3,128,256]{4,3,2,1,0:T(8,128)(2,1)S(1)}, bf16[10,2,3,128,256]{4,3,2,1,0:T(8,128)(2,1)}, u32[]{:S(2)}) copy-start(bf16[10,2,3,128,256]{4,3,2,1,0:T(8,128)(2,1)} %param.3) | copy-start | bytes 11796484
  6.5 6.2 %copy-start.1 = (bf16[10,2,3,256,256]{4,3,2,1,0:T(8,128)(2,1)S(1)}, bf16[10,2,3,256,256]{4,3,2,1,0:T(8,128)(2,1)}, u32[]{:S(2)}) copy-start(bf16[10,2,3,256,256]{4,3,2,1,0:T(8,128)(2,1)} %param.2) | copy-start | bytes 23592964
  19.5 39.3 %copy-start.2 = (u32[32]{0:T(128)S(1)}, u32[32]{0:T(128)}, u32[]{:S(2)}) copy-start(u32[32]{0:T(128)} %constant.21) | copy-start | bytes 388
Sparse Core Ops, SparseCore 0:
  19.7 103.5 all-reduce.2
where the time goes:
time: 132 us
  waiting for transfers between devices  63.2 us (48%)
  blocking collectives  36.2 us (27%)
  between operations  14.1 us (11%)
  matrix products  7.4 us (6%)
  local copies, waits for them, and re-layouts  6.04 us (5%)
  other arithmetic  4.94 us (4%)
    unnamed x2, waiting for transfers between devices  63.2 us
    psum x1, blocking collectives, shards(): totals = lax.psum(sumsq, ('blk', 'sol'))  36.2 us
    dot_general x1, matrix products, shards(): jnp.einsum('tckx,tcnx->ktn', eigvecs[:, 0], solutions[:, 1], preferred_el...  4.05 us
    another operation x1, local copies, waits for them, and re-layouts, shards(): jnp.stack((real, imag), axis=2)  3.25 us
    reduce_sum x1, other arithmetic, shards(): sumsq = jnp.sum(jnp.square(eigvecs.astype(jnp.float32)), axis=(1, 2, 4))  2.95 us
    unnamed x7, local copies, waits for them, and re-layouts  2.71 us
  transfers between devices with their start and end apart: 1, of which 1 were waited for; matrix products, arithmetic and copies ran while one was open for 3% of the time, Pallas kernels for 0%

commit v1 on v0

--- a/solution.py
+++ b/solution.py
@@ -1,10 +1,224 @@
+import functools
+
 import jax
 import jax.numpy as jnp
 from jax import lax
+from jax.experimental import pallas as pl
+from jax.experimental.pallas import tpu as pltpu
 from jax.sharding import PartitionSpec as P
 
-
-def shards(solutions, eigvecs):
+MESH = pl.DeviceIdType.MESH
+LANES = 128
+SUBLANES = 8
+
+
+def project_kernel(sizes, s_hbm, e_hbm, out, ev, sv, part, got1, got2, got3, nrm, ngot1, ngot2, ngot3,
+                   in_sem, snd1, rcv1, snd2, rcv2, snd3, rcv3, nsnd1, nrcv1, nsnd2, nrcv2, nsnd3, nrcv3):
+    slices, colors, rows, cols, chips_x, chips_z, own, floor_value = sizes
+    blk = lax.axis_index("blk")
+    sol = lax.axis_index("sol")
+    core = lax.rem(sol, 2)
+    x = sol // 2
+    other = 1 - core
+    partner = x * 2 + other
+
+    def x_at(d):
+        return lax.rem(x + d, chips_x)
+
+    def z_at(d):
+        return lax.rem(blk + d, chips_z)
+
+    def x_dev(d):
+        return {"sol": x_at(d) * 2 + core}
+
+    def z_dev(d):
+        return {"blk": z_at(d)}
+
+    barrier = pltpu.get_barrier_semaphore()
+    pl.semaphore_signal(barrier, inc=1, device_id={"sol": partner}, device_id_type=MESH)
+    for d in range(1, chips_x):
+        pl.semaphore_signal(barrier, inc=1, device_id=x_dev(d), device_id_type=MESH)
+    for d in range(1, chips_z):
+        pl.semaphore_signal(barrier, inc=1, device_id=z_dev(d), device_id_type=MESH)
+
+    def in_e(t):
+        return pltpu.make_async_copy(e_hbm.at[t], ev.at[t], in_sem.at[0, t])
+
+    def in_s(t):
+        return pltpu.make_async_copy(s_hbm.at[t], sv.at[t], in_sem.at[1, t])
+
+    def remote(src, dst, a, b, dev):
+        return pltpu.make_async_remote_copy(
+            src_ref=src, dst_ref=dst, send_sem=a, recv_sem=b, device_id=dev, device_id_type=MESH
+        )
+
+    def copy1(t):
+        return remote(part.at[t, other], got1.at[t], snd1.at[t], rcv1.at[t], {"sol": partner})
+
+    def copy2(t, d):
+        return remote(part.at[t, core, x_at(d)], got2.at[t, d - 1], snd2.at[t, d - 1], rcv2.at[t, d - 1], x_dev(d))
+
+    def copy3(t, d):
+        return remote(part.at[t, core, x, z_at(d)], got3.at[t, d - 1], snd3.at[t, d - 1], rcv3.at[t, d - 1], z_dev(d))
+
+    ncopy1 = remote(nrm.at[other], ngot1, nsnd1, nrcv1, {"sol": partner})
+
+    def ncopy2(d):
+        return remote(nrm.at[core, x_at(d)], ngot2.at[d - 1], nsnd2.at[d - 1], nrcv2.at[d - 1], x_dev(d))
+
+    def ncopy3(d):
+        return remote(nrm.at[core, x, z_at(d)], ngot3.at[d - 1], nsnd3.at[d - 1], nrcv3.at[d - 1], z_dev(d))
+
+    def start_in(t, _):
+        in_e(t).start()
+        in_s(t).start()
+        return 0
+
+    lax.fori_loop(0, slices, start_in, 0)
+    nrm[...] = jnp.zeros_like(nrm)
+
+    def compute(t):
+        in_e(t).wait()
+        in_s(t).wait()
+        total = None
+        squares = None
+        for c in range(colors):
+            a = ev[t, :, c]
+            b = sv[t, :, c]
+            a = a.reshape(2 * rows, a.shape[-1])
+            b = b.reshape(2 * cols, b.shape[-1])
+            p = lax.dot_general(a, b, (((1,), (1,)), ((), ())), preferred_element_type=jnp.float32)
+            total = p if total is None else total + p
+            wide = a.astype(jnp.float32)
+            wide = wide * wide
+            squares = wide if squares is None else squares + wide
+        real = total[:rows, :cols] + total[rows:, cols:]
+        imag = total[:rows, cols:] - total[rows:, :cols]
+        real = real.reshape(chips_z, chips_x, 2, own, cols)
+        imag = imag.reshape(chips_z, chips_x, 2, own, cols)
+        squares = jnp.sum(squares[:rows] + squares[rows:], axis=1, keepdims=True)
+        lane = lax.broadcasted_iota(jnp.int32, (rows, LANES), 1)
+        mark = jnp.where(lane == t, squares, 0.0).reshape(chips_z, chips_x, 2, own, LANES)
+        for k in range(2):
+            for i in range(chips_x):
+                part[t, k, i, :, :, :cols] = real[:, i, k]
+                part[t, k, i, :, :, cols:] = imag[:, i, k]
+                nrm[k, i] += mark[:, i, k]
+
+    def after1(t):
+        copy1(t).wait_recv()
+        part[t, core] += got1[t]
+        for d in range(1, chips_x):
+            copy2(t, d).start()
+
+    def after2(t):
+        for d in range(1, chips_x):
+            copy2(t, d).wait_recv()
+        part[t, core, x] += jnp.sum(got2[t], axis=0)
+        for d in range(1, chips_z):
+            copy3(t, d).start()
+
+    compute(0)
+    pl.semaphore_wait(barrier, 1 + (chips_x - 1) + (chips_z - 1))
+    copy1(0).start()
+
+    lag1, lag2 = 1, 3
+
+    def step(s, _):
+        compute(s)
+        copy1(s).start()
+
+        @pl.when(s >= lag1)
+        def _():
+            after1(s - lag1)
+
+        @pl.when(s >= lag2)
+        def _():
+            after2(s - lag2)
+
+        return 0
+
+    lax.fori_loop(1, slices, step, 0)
+    ncopy1.start()
+    for t in range(max(slices - lag1, 0), slices):
+        after1(t)
+    ncopy1.wait_recv()
+    nrm[core] += ngot1[...]
+    for d in range(1, chips_x):
+        ncopy2(d).start()
+    for t in range(max(slices - lag2, 0), slices):
+        after2(t)
+    for d in range(1, chips_x):
+        ncopy2(d).wait_recv()
+    nrm[core, x] += jnp.sum(ngot2[...], axis=0)
+    for d in range(1, chips_z):
+        ncopy3(d).start()
+    for d in range(1, chips_z):
+        ncopy3(d).wait_recv()
+    sums = nrm[core, x, blk] + jnp.sum(ngot3[...], axis=0)
+    scale = lax.rsqrt(jnp.maximum(sums, jnp.float32(floor_value)))
+    for t in range(slices):
+        for d in range(1, chips_z):
+            copy3(t, d).wait_recv()
+        done = (part[t, core, x, blk] + jnp.sum(got3[t], axis=0)) * scale[:, t : t + 1]
+        out[:, t, 0, :] = done[:, :cols]
+        out[:, t, 1, :] = done[:, cols:]
+
+    def drain(t, _):
+        copy1(t).wait_send()
+        for d in range(1, chips_x):
+            copy2(t, d).wait_send()
+        for d in range(1, chips_z):
+            copy3(t, d).wait_send()
+        return 0
+
+    lax.fori_loop(0, slices, drain, 0)
+    ncopy1.wait_send()
+    for d in range(1, chips_x):
+        ncopy2(d).wait_send()
+    for d in range(1, chips_z):
+        ncopy3(d).wait_send()
+
+
+def kernel_shards(chips_x, chips_z, solutions, eigvecs):
+    slices, parts, colors, rows, local = eigvecs.shape
+    cols = solutions.shape[3]
+    own = rows // (chips_x * 2 * chips_z)
+    sizes = (slices, colors, rows, cols, chips_x, chips_z, own, local * chips_x * 2 * chips_z)
+    f32 = jnp.float32
+    dma = pltpu.SemaphoreType.DMA
+    wide = 2 * cols
+    return pl.pallas_call(
+        functools.partial(project_kernel, sizes),
+        out_shape=jax.ShapeDtypeStruct((own, slices, 2, cols), f32),
+        in_specs=[pl.BlockSpec(memory_space=pl.ANY)] * 2,
+        out_specs=pl.BlockSpec(memory_space=pltpu.VMEM),
+        scratch_shapes=[
+            pltpu.VMEM(eigvecs.shape, eigvecs.dtype),
+            pltpu.VMEM(solutions.shape, solutions.dtype),
+            pltpu.VMEM((slices, 2, chips_x, chips_z, own, wide), f32),
+            pltpu.VMEM((slices, chips_x, chips_z, own, wide), f32),
+            pltpu.VMEM((slices, chips_x - 1, chips_z, own, wide), f32),
+            pltpu.VMEM((slices, chips_z - 1, own, wide), f32),
+            pltpu.VMEM((2, chips_x, chips_z, own, LANES), f32),
+            pltpu.VMEM((chips_x, chips_z, own, LANES), f32),
+            pltpu.VMEM((chips_x - 1, chips_z, own, LANES), f32),
+            pltpu.VMEM((chips_z - 1, own, LANES), f32),
+            dma((2, slices)),
+            dma((slices,)), dma((slices,)),
+            dma((slices, chips_x - 1)), dma((slices, chips_x - 1)),
+            dma((slices, chips_z - 1)), dma((slices, chips_z - 1)),
+            dma, dma,
+            dma((chips_x - 1,)), dma((chips_x - 1,)),
+            dma((chips_z - 1,)), dma((chips_z - 1,)),
+        ],
+        compiler_params=pltpu.CompilerParams(
+            collective_id=0, has_side_effects=True, vmem_limit_bytes=60 * 1024 * 1024
+        ),
+    )(solutions, eigvecs)
+
+
+def plain_shards(solutions, eigvecs):
     blocks = lax.axis_size("blk")
     within = lax.axis_size("sol")
     slices, _, _, total_rows, local_sites = eigvecs.shape
@@ -29,6 +243,15 @@
 
 
 def solution(mesh):
+    blocks, within = mesh.shape["blk"], mesh.shape["sol"]
+
+    def shards(solutions, eigvecs):
+        slices, rows = eigvecs.shape[0], eigvecs.shape[3]
+        own = rows // (blocks * within)
+        if own % SUBLANES or within % 2 or within < 4 or blocks < 2 or slices > LANES:
+            return plain_shards(solutions, eigvecs)
+        return kernel_shards(within // 2, blocks, solutions, eigvecs)
+
     in_specs = (
         P("cuts", None, None, None, ("blk", "sol")),
         P("cuts", None, None, None, ("blk", "sol")),

time: 132 us -> 31.2 us (0.24)
  waiting for transfers between devices: 63.2 us -> 0 us
  blocking collectives: 36.2 us -> 0 us
  Pallas kernels: 0 us -> 29.4 us
  between operations: 14.1 us -> 0.01 us
  matrix products: 7.4 us -> 0 us
  other arithmetic: 4.94 us -> 0 us
  local copies, waits for them, and re-layouts: 6.04 us -> 1.59 us
    unnamed x2 -> x0, waiting for transfers between devices: 63.2 us -> none
    psum x1 -> x0, blocking collectives: 36.2 us -> none  [shards(): totals = lax.psum(sumsq, ('blk', 'sol'))]
    pallas_call x0 -> x1, Pallas kernels: none -> 29.4 us  [kernel_shards(): pl.pallas_call(functools.partial(project_kernel, sizes), out_shape=jax.Sh...]
    dot_general x3 -> x0, matrix products: 7.4 us -> none  [the longest x1 4.05 us: shards(): jnp.einsum('tckx,tcnx->ktn', eigvecs[:, 0], solutions[:, 1], preferred_el...]
    another operation x1 -> x0, local copies, waits for them, and re-layouts: 3.25 us -> none  [shards(): jnp.stack((real, imag), axis=2)]
    reduce_sum x1 -> x0, other arithmetic: 2.95 us -> none  [shards(): sumsq = jnp.sum(jnp.square(eigvecs.astype(jnp.float32)), axis=(1, 2, 4))]
    mul x1 -> x0, other arithmetic: 1.73 us -> none  [shards(): return summed * jnp.transpose(mine)[:, :, None, None]]
    unnamed x7 -> x1, local copies, waits for them, and re-layouts: 2.71 us -> 1.59 us
  transfers between devices with their start and end apart: 1 -> 0, of which waited for: 1 -> 0; matrix products, arithmetic and copies ran while one was open for 3% -> 0% of each run, Pallas kernels for 0% -> 0%
where the time goes in v1:
time: 31.2 us; the launch traced here: 31 us
  Pallas kernels  29.4 us (94%)
  local copies, waits for them, and re-layouts  1.59 us (5%)
    pallas_call x1, Pallas kernels, kernel_shards(): pl.pallas_call(functools.partial(project_kernel, sizes), out_shape=jax.Sh...  29.4 us
    unnamed x1, local copies, waits for them, and re-layouts  1.59 us

profile of v1, /device:TPU:0, one launch (start us, length us, event | category | flops | bytes accessed | tf_op | source)
XLA Modules:
  0.0 31.0 jit_solution(14228555906605697714)
XLA Ops:
  0.0 29.4 %shard_map.28 = f32[8,10,2,256]{3,2,1,0:T(2,128)} custom-call(bf16[10,2,3,256,256]{4,3,2,1,0:T(8,128)(2,1)} %s_hbm.1, bf16[10,2,3,128,256]{4,3,2,1,0:T(8,128)(2,1)} %e_hbm.1), custom_call_target="tpu_custom_call" | custom-call | tf_op jit(solution)/shard_map/pallas_call | solution.py:191
  29.4 1.6 %copy.4 = f32[8,10,2,256]{3,2,1,0:T(2,128)} copy(f32[8,10,2,256]{3,2,1,0:T(2,128)} %shard_map.28) | data formatting | bytes 327680

commit v2 on v1

v2 whole, which is shorter than its diff:
```python
import functools

import jax
import jax.numpy as jnp
from jax import lax
from jax.experimental import pallas as pl
from jax.experimental.pallas import tpu as pltpu
from jax.sharding import PartitionSpec as P

MESH = pl.DeviceIdType.MESH
LANES = 128
SUBLANES = 8
EARLY_B = 3
LAG = 3
LAG2 = 1


def plan_of(slices):
    early = 2 * EARLY_B
    return "".join("B" if t < early and t % 2 else "A" for t in range(slices - 1)) + "D"


def project_kernel(sizes, s_hbm, e_hbm, out, ev, sv, part, got1, gotx, gotl, goth, gotbl, gotbx, gotd, nrm, ngot1, ngot2, ngot3,
                   in_sem, snd1, rcv1, sndx, rcvx, sndl, rcvl, sndh, rcvh, sndd, rcvd,
                   nsnd1, nrcv1, nsnd2, nrcv2, nsnd3, nrcv3):
    slices, colors, rows, cols, chips_x, chips_z, own, floor_value = sizes
    plan = plan_of(slices)
    high = chips_z // 2
    blk = lax.axis_index("blk")
    sol = lax.axis_index("sol")
    core = lax.rem(sol, 2)
    x = sol // 2
    l = lax.rem(blk, 2)
    h = blk // 2
    other = 1 - core
    partner = {"sol": x * 2 + other}
    beside = {"blk": h * 2 + 1 - l}

    def x_at(d):
        return lax.rem(x + d, chips_x)

    def h_at(d):
        return lax.rem(h + d, high)

    def z_at(d):
        return lax.rem(blk + d, chips_z)

    def x_dev(d):
        return {"sol": x_at(d) * 2 + core}

    def h_dev(d):
        return {"blk": h_at(d) * 2 + l}

    def z_dev(d):
        return {"blk": z_at(d)}

    xs, hs, zs = range(1, chips_x), range(1, high), range(1, chips_z)

    barrier = pltpu.get_barrier_semaphore()
    pl.semaphore_signal(barrier, inc=1, device_id=partner, device_id_type=MESH)
    for d in xs:
        pl.semaphore_signal(barrier, inc=1, device_id=x_dev(d), device_id_type=MESH)
    for d in zs:
        pl.semaphore_signal(barrier, inc=1, device_id=z_dev(d), device_id_type=MESH)

    def in_e(t):
        return pltpu.make_async_copy(e_hbm.at[t], ev.at[t], in_sem.at[0, t])

    def in_s(t):
        return pltpu.make_async_copy(s_hbm.at[t], sv.at[t], in_sem.at[1, t])

    started = []

    def remote(src, dst, a, b, dev):
        return pltpu.make_async_remote_copy(
            src_ref=src, dst_ref=dst, send_sem=a, recv_sem=b, device_id=dev, device_id_type=MESH
        )

    def go(copies):
        for copy in copies:
            copy.start()
            started.append(copy)

    def arrive(copies):
        for copy in copies:
            copy.wait_recv()

    def core_copies(t):
        return [remote(part.at[t, other], got1.at[t], snd1.at[t], rcv1.at[t], partner)]

    def x_copies(t):
        if plan[t] == "B":
            slot = plan[:t].count("B")
            return [remote(part.at[t, core, x_at(d), l], gotbx.at[slot, d - 1], sndx.at[t, d - 1], rcvx.at[t, d - 1], x_dev(d)) for d in xs]
        return [remote(part.at[t, core, x_at(d)], gotx.at[t, d - 1], sndx.at[t, d - 1], rcvx.at[t, d - 1], x_dev(d)) for d in xs]

    def low_copies(t):
        if plan[t] == "B":
            slot = plan[:t].count("B")
            return [remote(part.at[t, core, :, 1 - l], gotbl.at[slot], sndl.at[t], rcvl.at[t], beside)]
        return [remote(part.at[t, core, x, 1 - l], gotl.at[t], sndl.at[t], rcvl.at[t], beside)]

    def high_copies(t):
        if plan[t] == "D":
            return [remote(part.at[t, core, x, lax.rem(z_at(d), 2), z_at(d) // 2], gotd.at[d - 1], sndd.at[d - 1], rcvd.at[d - 1], z_dev(d)) for d in zs]
        return [remote(part.at[t, core, x, l, h_at(d)], goth.at[t, d - 1], sndh.at[t, d - 1], rcvh.at[t, d - 1], h_dev(d)) for d in hs]

    ncopy1 = [remote(nrm.at[other], ngot1, nsnd1, nrcv1, partner)]
    ncopy2 = [remote(nrm.at[core, x_at(d)], ngot2.at[d - 1], nsnd2.at[d - 1], nrcv2.at[d - 1], x_dev(d)) for d in xs]
    ncopy3 = [remote(nrm.at[core, x, lax.rem(z_at(d), 2), z_at(d) // 2], ngot3.at[d - 1], nsnd3.at[d - 1], nrcv3.at[d - 1], z_dev(d)) for d in zs]

    def start_in(t, _):
        in_e(t).start()
        in_s(t).start()
        return 0

    lax.fori_loop(0, slices, start_in, 0)
    nrm[...] = jnp.zeros_like(nrm)

    def compute(t):
        in_e(t).wait()
        in_s(t).wait()
        total = None
        squares = None
        for c in range(colors):
            a = ev[t, :, c]
            b = sv[t, :, c]
            a = a.reshape(2 * rows, a.shape[-1])
            b = b.reshape(2 * cols, b.shape[-1])
            p = lax.dot_general(a, b, (((1,), (1,)), ((), ())), preferred_element_type=jnp.float32)
            total = p if total is None else total + p
            wide = a.astype(jnp.float32)
            wide = wide * wide
            squares = wide if squares is None else squares + wide
        real = total[:rows, :cols] + total[rows:, cols:]
        imag = total[:rows, cols:] - total[rows:, :cols]
        real = real.reshape(high, 2, chips_x, 2, own, cols)
        imag = imag.reshape(high, 2, chips_x, 2, own, cols)
        squares = jnp.sum(squares[:rows] + squares[rows:], axis=1, keepdims=True)
        lane = lax.broadcasted_iota(jnp.int32, (rows, LANES), 1)
        mark = jnp.where(lane == t, squares, 0.0).reshape(high, 2, chips_x, 2, own, LANES)
        for k in range(2):
            for i in range(chips_x):
                for j in range(2):
                    part[t, k, i, j, :, :, :cols] = real[:, j, i, k]
                    part[t, k, i, j, :, :, cols:] = imag[:, j, i, k]
                    nrm[k, i, j] += mark[:, j, i, k]

    def after_core(t):
        arrive(core_copies(t))
        part[t, core] += got1[t]
        go(low_copies(t) if plan[t] == "B" else x_copies(t))

    def after_first(t):
        if plan[t] == "B":
            arrive(low_copies(t))
            part[t, core, :, l] += gotbl[plan[:t].count("B")]
            go(x_copies(t))
        else:
            arrive(x_copies(t))
            part[t, core, x] += jnp.sum(gotx[t], axis=0)
            go(high_copies(t) if plan[t] == "D" else low_copies(t))

    def after_second(t):
        if plan[t] == "B":
            arrive(x_copies(t))
            part[t, core, x, l] += jnp.sum(gotbx[plan[:t].count("B")], axis=0)
            go(high_copies(t))
        elif plan[t] == "A":
            arrive(low_copies(t))
            part[t, core, x, l] += gotl[t]
            go(high_copies(t))

    last = slices - 1
    for t in range(slices):
        compute(t)
        if t == 0:
            pl.semaphore_wait(barrier, 1 + (chips_x - 1) + (chips_z - 1))
        if t == last:
            go(ncopy1)
        go(core_copies(t))
        if t >= 1:
            after_core(t - 1)
        if t >= LAG:
            after_first(t - LAG)
        if t >= LAG + LAG2:
            after_second(t - LAG - LAG2)
    arrive(ncopy1)
    nrm[core] += ngot1[...]
    go(ncopy2)
    after_core(last)
    for s in range(slices, slices + LAG + LAG2):
        if s == last + LAG:
            arrive(ncopy2)
            nrm[core, x] += jnp.sum(ngot2[...], axis=0)
            go(ncopy3)
        if 0 <= s - LAG < slices:
            after_first(s - LAG)
        if 0 <= s - LAG - LAG2 < slices:
            after_second(s - LAG - LAG2)
    arrive(ncopy3)
    sums = nrm[core, x, l, h] + jnp.sum(ngot3[...], axis=0)
    scale = lax.rsqrt(jnp.maximum(sums, jnp.float32(floor_value)))
    for t in range(slices):
        arrive(high_copies(t))
        extra = jnp.sum(gotd[...] if plan[t] == "D" else goth[t], axis=0)
        done = (part[t, core, x, l, h] + extra) * scale[:, t : t + 1]
        out[:, t, 0, :] = done[:, :cols]
        out[:, t, 1, :] = done[:, cols:]
    for copy in started:
        copy.wait_send()


def kernel_shards(chips_x, chips_z, solutions, eigvecs):
    slices, parts, colors, rows, local = eigvecs.shape
    cols = solutions.shape[3]
    own = rows // (chips_x * 2 * chips_z)
    high = chips_z // 2
    bees = max(plan_of(slices).count("B"), 1)
    sizes = (slices, colors, rows, cols, chips_x, chips_z, own, local * chips_x * 2 * chips_z)
    f32 = jnp.float32
    dma = pltpu.SemaphoreType.DMA
    wide = 2 * cols
    return pl.pallas_call(
        functools.partial(project_kernel, sizes),
        out_shape=jax.ShapeDtypeStruct((own, slices, 2, cols), f32),
        in_specs=[pl.BlockSpec(memory_space=pl.ANY)] * 2,
        out_specs=pl.BlockSpec(memory_space=pltpu.VMEM),
        scratch_shapes=[
            pltpu.VMEM(eigvecs.shape, eigvecs.dtype),
            pltpu.VMEM(solutions.shape, solutions.dtype),
            pltpu.VMEM((slices, 2, chips_x, 2, high, own, wide), f32),
            pltpu.VMEM((slices, chips_x, 2, high, own, wide), f32),
            pltpu.VMEM((slices, chips_x - 1, 2, high, own, wide), f32),
            pltpu.VMEM((slices, high, own, wide), f32),
            pltpu.VMEM((slices, high - 1, own, wide), f32),
            pltpu.VMEM((bees, chips_x, high, own, wide), f32),
            pltpu.VMEM((bees, chips_x - 1, high, own, wide), f32),
            pltpu.VMEM((chips_z - 1, own, wide), f32),
            pltpu.VMEM((2, chips_x, 2, high, own, LANES), f32),
            pltpu.VMEM((chips_x, 2, high, own, LANES), f32),
            pltpu.VMEM((chips_x - 1, 2, high, own, LANES), f32),
            pltpu.VMEM((chips_z - 1, own, LANES), f32),
            dma((2, slices)),
            dma((slices,)), dma((slices,)),
            dma((slices, chips_x - 1)), dma((slices, chips_x - 1)),
            dma((slices,)), dma((slices,)),
            dma((slices, high - 1)), dma((slices, high - 1)),
            dma((chips_z - 1,)), dma((chips_z - 1,)),
            dma, dma,
            dma((chips_x - 1,)), dma((chips_x - 1,)),
            dma((chips_z - 1,)), dma((chips_z - 1,)),
        ],
        compiler_params=pltpu.CompilerParams(
            collective_id=0, has_side_effects=True, vmem_limit_bytes=60 * 1024 * 1024
        ),
    )(solutions, eigvecs)


def plain_shards(solutions, eigvecs):
    blocks = lax.axis_size("blk")
    within = lax.axis_size("sol")
    slices, _, _, total_rows, local_sites = eigvecs.shape
    sumsq = jnp.sum(jnp.square(eigvecs.astype(jnp.float32)), axis=(1, 2, 4))
    totals = lax.psum(sumsq, ("blk", "sol"))
    floor_value = jnp.float32(local_sites * blocks * within)
    scale = lax.rsqrt(jnp.maximum(totals, floor_value))
    own_rows = total_rows // (blocks * within)
    real = jnp.einsum("trckx,trcnx->ktn", eigvecs, solutions, preferred_element_type=jnp.float32)
    imag = jnp.einsum(
        "tckx,tcnx->ktn", eigvecs[:, 0], solutions[:, 1], preferred_element_type=jnp.float32
    )
    imag = imag - jnp.einsum(
        "tckx,tcnx->ktn", eigvecs[:, 1], solutions[:, 0], preferred_element_type=jnp.float32
    )
    summed = lax.psum_scatter(
        jnp.stack((real, imag), axis=2), ("blk", "sol"), scatter_dimension=0, tiled=True
    )
    owner = lax.axis_index("blk") * within + lax.axis_index("sol")
    mine = lax.dynamic_slice_in_dim(scale, owner * own_rows, own_rows, 1)
    return summed * jnp.transpose(mine)[:, :, None, None]


def solution(mesh):
    blocks, within = mesh.shape["blk"], mesh.shape["sol"]

    def shards(solutions, eigvecs):
        slices, rows = eigvecs.shape[0], eigvecs.shape[3]
        own = rows // (blocks * within)
        if own % SUBLANES or within % 2 or within < 4 or blocks % 2 or blocks < 4 or slices < 2 or slices > LANES:
            return plain_shards(solutions, eigvecs)
        return kernel_shards(within // 2, blocks, solutions, eigvecs)

    in_specs = (
        P("cuts", None, None, None, ("blk", "sol")),
        P("cuts", None, None, None, ("blk", "sol")),
    )
    out_specs = P(("blk", "sol"), "cuts", None, None)
    return jax.shard_map(shards, mesh=mesh, in_specs=in_specs, out_specs=out_specs, check_vma=False)
```

time: 31.2 us -> 34.3 us (1.099)
  Pallas kernels: 29.4 us -> 32.6 us
    pallas_call x1, Pallas kernels: 29.4 us -> 32.6 us  [kernel_shards(): pl.pallas_call(functools.partial(project_kernel, sizes), out_shape=jax.Sh...]
where the time goes in v2:
time: 34.3 us; the launch traced here: 34.2 us
  Pallas kernels  32.6 us (95%)
  local copies, waits for them, and re-layouts  1.59 us (5%)
    pallas_call x1, Pallas kernels, kernel_shards(): pl.pallas_call(functools.partial(project_kernel, sizes), out_shape=jax.Sh...  32.6 us
    unnamed x1, local copies, waits for them, and re-layouts  1.59 us

profile of v2, /device:TPU:0, one launch (start us, length us, event | category | flops | bytes accessed | tf_op | source)
XLA Modules:
  0.0 34.2 jit_solution(12980887282242863572)
XLA Ops:
  0.0 32.6 %shard_map.28 = f32[8,10,2,256]{3,2,1,0:T(2,128)} custom-call(bf16[10,2,3,256,256]{4,3,2,1,0:T(8,128)(2,1)} %s_hbm.1, bf16[10,2,3,128,256]{4,3,2,1,0:T(8,128)(2,1)} %e_hbm.1), custom_call_target="tpu_custom_call" | custom-call | tf_op jit(solution)/shard_map/pallas_call | solution.py:224
  32.6 1.6 %copy.4 = f32[8,10,2,256]{3,2,1,0:T(2,128)} copy(f32[8,10,2,256]{3,2,1,0:T(2,128)} %shard_map.28) | data formatting | bytes 327680

commit v3 on v2

--- a/solution.py
+++ b/solution.py
@@ -11,8 +11,9 @@
 LANES = 128
 SUBLANES = 8
 EARLY_B = 3
-LAG = 3
-LAG2 = 1
+LAG = 6
+LAG2 = 4
+AHEAD = 3
 
 
 def plan_of(slices):
@@ -109,17 +110,18 @@
     ncopy2 = [remote(nrm.at[core, x_at(d)], ngot2.at[d - 1], nsnd2.at[d - 1], nrcv2.at[d - 1], x_dev(d)) for d in xs]
     ncopy3 = [remote(nrm.at[core, x, lax.rem(z_at(d), 2), z_at(d) // 2], ngot3.at[d - 1], nsnd3.at[d - 1], nrcv3.at[d - 1], z_dev(d)) for d in zs]
 
-    def start_in(t, _):
+    def start_in(t):
         in_e(t).start()
         in_s(t).start()
-        return 0
-
-    lax.fori_loop(0, slices, start_in, 0)
+
+    start_in(0)
     nrm[...] = jnp.zeros_like(nrm)
 
     def compute(t):
         in_e(t).wait()
         in_s(t).wait()
+        for ahead in range(t + AHEAD if t else 1, min(t + AHEAD + 1, slices)):
+            start_in(ahead)
         total = None
         squares = None
         for c in range(colors):
@@ -252,7 +254,7 @@
             dma((chips_z - 1,)), dma((chips_z - 1,)),
         ],
         compiler_params=pltpu.CompilerParams(
-            collective_id=0, has_side_effects=True, vmem_limit_bytes=60 * 1024 * 1024
+            collective_id=0, has_side_effects=True, vmem_limit_bytes=52 * 1024 * 1024
         ),
     )(solutions, eigvecs)
 

time: 34.3 us -> 29.9 us (0.87)
  Pallas kernels: 32.6 us -> 29.1 us
  local copies, waits for them, and re-layouts: 1.59 us -> 0.67 us
    pallas_call x1, Pallas kernels: 32.6 us -> 29.1 us  [kernel_shards(): pl.pallas_call(functools.partial(project_kernel, sizes), out_shape=jax.Sh...]
    unnamed x1, local copies, waits for them, and re-layouts: 1.59 us -> 0.67 us
where the time goes in v3:
time: 29.9 us; the launch traced here: 29.7 us
  Pallas kernels  29.1 us (97%)
  local copies, waits for them, and re-layouts  0.67 us (2%)
    pallas_call x1, Pallas kernels, kernel_shards(): pl.pallas_call(functools.partial(project_kernel, sizes), out_shape=jax.Sh...  29.1 us
    unnamed x1, local copies, waits for them, and re-layouts  0.67 us

profile of v3, /device:TPU:0, one launch (start us, length us, event | category | flops | bytes accessed | tf_op | source)
XLA Modules:
  0.0 29.7 jit_solution(7942944874600870337)
XLA Ops:
  0.0 29.1 %shard_map.28 = f32[8,10,2,256]{3,2,1,0:T(2,128)S(1)} custom-call(bf16[10,2,3,256,256]{4,3,2,1,0:T(8,128)(2,1)} %s_hbm.1, bf16[10,2,3,128,256]{4,3,2,1,0:T(8,128)(2,1)} %e_hbm.1), custom_call_target="tpu_custom_call" | custom-call | tf_op jit(solution)/shard_map/pallas_call | solution.py:226
  29.1 0.7 %copy.4 = f32[8,10,2,256]{3,2,1,0:T(2,128)} copy(f32[8,10,2,256]{3,2,1,0:T(2,128)S(1)} %shard_map.28) | data formatting | bytes 327680
